TPU v7x, 32 devices: a whole 2x2x4 slice. The times are simulated.
32 devices in a mesh: row: 8 (over z, x), col: 4 (over y, core).
Axes of the slice: x: 2, y: 2, z: 4, core: 2. Of those that a mesh axis runs over, the one named last changes fastest.
Arguments:
- left: bfloat16 [128, 4096], P('col', 'row'), may hold values from -6 to 6
- right: bfloat16 [128, 4096], P('row', 'col'), may hold values from -6 to 6
- pair_in: bfloat16 [128, 128, 128], P('row', 'col'), may hold values from -6 to 6
- pair_cot: bfloat16 [128, 128, 128], P('row', 'col'), may hold values from -6 to 6
- ln_gain: float32 [128], replicated, may hold values from 0.25 to 1.75
- out_weight: bfloat16 [1024, 128], replicated, may hold values from -2 to 2
- out_bias: float32 [128], replicated, may hold values from -3 to 3
- trans_up: bfloat16 [128, 512], replicated, may hold values from -0.5 to 0.5
- trans_down: bfloat16 [512, 128], replicated, may hold values from -0.25 to 0.25
Outputs:
- pair_out: bfloat16 [128, 128, 128], P('row', 'col')
- grad_left: bfloat16 [128, 4096], P('col', 'row')
- grad_right: bfloat16 [128, 4096], P('row', 'col')
All inputs are finite; a program needn't handle non-finite values.
Results may differ from a plain program's by a relative error of at most 0.01.
The roundings to bfloat16 on the way count: a program that leaves them out, or rounds other values in their place, can miss the bound.
Values may be sent and summed in bfloat16 or wider, within the bound.
A program may use at most 64 MiB of HBM per device.

v0:
```python
import jax
import jax.numpy as jnp
from jax import lax
from jax.sharding import PartitionSpec as P

C = 32
SEQS = 128


def pair_block(outer, pair_in, pair_cot, ln_gain, out_weight, out_bias, trans_up, trans_down):
    update = jnp.einsum("ijk,kd->ijd", outer, out_weight, preferred_element_type=jnp.float32)
    middle = pair_in.astype(jnp.float32) + update + out_bias
    centre = jnp.mean(middle, axis=-1, keepdims=True)
    centred = middle - centre
    spread = jnp.mean(centred * centred, axis=-1, keepdims=True)
    inverse = lax.rsqrt(spread + 1e-05)
    normal_x = centred * inverse
    normed = (normal_x * ln_gain).astype(jnp.bfloat16)
    preact = jnp.einsum("ijk,kf->ijf", normed, trans_up, preferred_element_type=jnp.float32)
    hidden = jnp.maximum(preact, 0.0).astype(jnp.bfloat16)
    down = jnp.einsum("ijf,fk->ijk", hidden, trans_down, preferred_element_type=jnp.float32)
    pair_out = (middle + down).astype(jnp.bfloat16)
    back = jnp.einsum("ijk,fk->ijf", pair_cot, trans_down, preferred_element_type=jnp.float32)
    d_hidden = jnp.where(preact > 0.0, back, 0.0).astype(jnp.bfloat16)
    d_normed = jnp.einsum("ijf,kf->ijk", d_hidden, trans_up, preferred_element_type=jnp.float32)
    scaled = d_normed * ln_gain
    d_middle = pair_cot.astype(jnp.float32) + inverse * (
        scaled
        - jnp.mean(scaled, axis=-1, keepdims=True)
        - normal_x * jnp.mean(scaled * normal_x, axis=-1, keepdims=True)
    )
    d_middle = d_middle.astype(jnp.bfloat16)
    d_outer = jnp.einsum("ijk,ck->ijc", d_middle, out_weight, preferred_element_type=jnp.float32)
    return (pair_out, d_outer.astype(jnp.bfloat16))


def on_device(left, right, pair_in, pair_cot, ln_gain, out_weight, out_bias, trans_up, trans_down):
    row_count = pair_in.shape[0]
    col_count = pair_in.shape[1]
    left_all = lax.all_gather(left, "col", axis=0, tiled=True)
    left_rows = left_all.reshape(SEQS, row_count, C)
    right_all = lax.all_gather(right, "row", axis=0, tiled=True)
    summed = jnp.einsum(
        "sic,sje->ijce",
        left_rows,
        right_all.reshape(SEQS, col_count, C),
        preferred_element_type=jnp.float32,
    )
    outer = (summed * (1.0 / SEQS)).astype(jnp.bfloat16).reshape(row_count, col_count, C * C)
    pair_out, d_outer = pair_block(
        outer, pair_in, pair_cot, ln_gain, out_weight, out_bias, trans_up, trans_down
    )
    grad_tiles = d_outer.reshape(row_count, col_count, C, C)
    right_cols = right_all.reshape(SEQS, col_count, C)
    product = jnp.einsum("ijce,sic->sje", grad_tiles, left_rows, preferred_element_type=jnp.float32)
    right_total = lax.psum_scatter(
        product.reshape(lax.axis_size("row") * right.shape[0], col_count * C),
        "row",
        scatter_dimension=0,
        tiled=True,
    )
    product = jnp.einsum(
        "ijce,sje->sic", grad_tiles, right_cols, preferred_element_type=jnp.float32
    )
    left_total = lax.psum_scatter(
        product.reshape(lax.axis_size("col") * left.shape[0], row_count * C),
        "col",
        scatter_dimension=0,
        tiled=True,
    )
    grad_left = (left_total * (1.0 / SEQS)).astype(jnp.bfloat16)
    grad_right = (right_total * (1.0 / SEQS)).astype(jnp.bfloat16)
    return (pair_out, grad_left, grad_right)


def solution(mesh):
    return jax.shard_map(
        on_device,
        mesh=mesh,
        in_specs=(
            P("col", "row"),
            P("row", "col"),
            P("row", "col", None),
            P("row", "col", None),
            P(),
            P(),
            P(),
            P(),
            P(),
        ),
        out_specs=(P("row", "col", None), P("col", "row"), P("row", "col")),
        check_vma=False,
    )
```

profile of v0, /device:TPU:0, one launch (start us, length us, event | category | flops | bytes accessed | tf_op | source)
XLA Modules:
  0.0 168.9 jit_solution(14177466887783532117)
XLA Ops:
  7.2 0.0 copy-start
  7.2 0.0 reduce-scatter.3.cloned.1.call-start
  7.2 6.9 %all_gather.7 = bf16[128,512]{1,0:T(8,128)(2,1)S(1)} all-gather(bf16[32,512]{1,0:T(8,128)(2,1)} %param.9), channel_id=1, replica_groups=mesh['row'=8,'col'=4] {'col'}, dimensions={0}, use_global_device_ids=true | all-gather | bytes 163840 | tf_op jit(solution)/shard_map/all_gather | solution.py:40
  14.1 0.1 copy.20
  14.2 31.8 %all_gather.6 = bf16[128,1024]{1,0:T(8,128)(2,1)S(1)} all-gather(bf16[16,1024]{1,0:T(8,128)(2,1)} %param.10), channel_id=1, replica_groups=mesh['row'=8,'col'=4] {'row'}, dimensions={0}, use_global_device_ids=true | all-gather | bytes 294912 | tf_op jit(solution)/shard_map/all_gather | solution.py:42
  46.0 0.2 copy.19
  46.2 3.2 %fusion = bf16[16,32,32,32]{2,3,0,1:T(8,128)(2,1)} fusion(bf16[128,32,32,1]{0,2,3,1:T(8,128)(2,1)S(1)} %bitcast.58, bf16[128,16,32,1]{0,2,1,3:T(8,128)(2,1)S(1)} %bitcast.60), kind=kOutput, calls=%fused_computation.1 | convolution fusion | flops 135266304 | bytes 1441792 | tf_op jit(solution)/shard_map/sic,sje->ijce/dot_general | solution.py:43
  49.4 6.4 %copy.21 = bf16[16,32,32,32]{3,2,1,0:T(8,128)(2,1)} copy(bf16[16,32,32,32]{2,3,0,1:T(8,128)(2,1)} %fusion) | data formatting | bytes 2097152 | tf_op jit(solution)/shard_map/convert_element_type | solution.py:49
  55.7 0.0 copy-start.1
  55.7 0.0 copy-start.4
  55.7 0.0 copy-start.5
  55.7 0.0 copy-start.6
  55.7 0.0 copy-start.2
  55.7 0.0 copy-start.3
  55.7 6.3 %reshape.49 = bf16[16,32,1024]{2,1,0:T(8,128)(2,1)S(1)} reshape(bf16[16,32,32,32]{3,2,1,0:T(8,128)(2,1)} %copy.21) | data formatting | bytes 2097152 | tf_op jit(solution)/shard_map/reshape | solution.py:49
  62.0 0.0 copy-done
  62.0 0.0 copy-done.1
  62.0 0.0 copy-done.4
  62.0 0.5 fusion.27
  62.6 0.3 multiply_reduce_fusion.1
  62.8 0.0 copy-done.5
  62.9 0.0 copy-done.6
  62.9 0.4 fusion.6
  63.2 0.3 and_convert_fusion
  63.5 0.0 copy-done.2
  63.5 0.0 copy-done.3
  63.5 0.6 fusion.26
  64.2 0.6 convolution_convert_fusion
  64.8 4.4 %reshape.50 = bf16[16,32,32,32]{3,2,1,0:T(8,128)(2,1)} reshape(bf16[16,32,1024]{2,1,0:T(8,128)(2,1)S(1)} %convolution_convert_fusion) | data formatting | bytes 2097152 | tf_op jit(solution)/shard_map/reshape | solution.py:53
  69.2 3.1 %fusion.30 = f32[16,32,128,1]{2,1,3,0:T(8,128)S(1)} fusion(bf16[16,32,32,32]{3,2,1,0:T(8,128)(2,1)} %reshape.50, bf16[128,32,32,1]{0,2,1,3:T(8,128)(2,1)S(1)} %bitcast.59), kind=kOutput, calls=%fused_computation.46 | convolution fusion | flops 134217728 | bytes 1572864 | tf_op jit(solution)/shard_map/ijce,sje->sic/dot_general | solution.py:62
  72.3 0.8 copy.24
  73.1 0.0 reduce-scatter.3.cloned.1.call-update
  73.1 0.0 reduce-scatter.5.cloned.1.call-start
  73.2 3.4 %fusion.31 = f32[32,32,128,1]{2,1,0,3:T(8,128)S(1)} fusion(bf16[16,32,32,32]{3,2,1,0:T(8,128)(2,1)} %reshape.50, bf16[128,16,32,1]{0,2,3,1:T(8,128)(2,1)S(1)} %bitcast.61), kind=kOutput, calls=%fused_computation.47 | convolution fusion | flops 134217728 | bytes 1703936 | tf_op jit(solution)/shard_map/ijce,sic->sje/dot_general | solution.py:55
  76.6 1.0 copy.26
  77.6 0.0 reduce-scatter.5.cloned.1.call-update
  77.6 1.0 fusion.5
  78.6 15.5 %reduce-scatter.3.cloned.1.call-done = f32[32,512]{1,0:T(8,128)} async-done(((f32[128,512]{1,0:T(8,128)}), f32[32,512]{1,0:T(8,128)}) %reduce-scatter.3.cloned.1.call-update) | async-done | bytes 65552 | tf_op jit(solution)/shard_map/reduce_scatter | solution.py:65
  94.1 1.5 multiply_convert_fusion.4
  95.6 65.0 %reduce-scatter.5.cloned.1.call-done = f32[16,1024]{1,0:T(8,128)} async-done(((f32[128,1024]{1,0:T(8,128)}), f32[16,1024]{1,0:T(8,128)}) %reduce-scatter.5.cloned.1.call-update) | async-done | bytes 65552 | tf_op jit(solution)/shard_map/reduce_scatter | solution.py:56
  160.6 1.5 multiply_convert_fusion.3
  (3 shorter events, 0.0 us)
Async XLA Ops:
  7.2 54.8 %copy-start = (bf16[1024,128]{1,0:T(8,128)(2,1)S(1)}, bf16[1024,128]{1,0:T(8,128)(2,1)}, u32[]{:S(2)}) copy-start(bf16[1024,128]{1,0:T(8,128)(2,1)} %param.14) | copy-start | bytes 786436
  7.2 86.9 %reduce-scatter.3.cloned.1.call-start = ((), (), s32[]{:S(2)}) async-start(), calls=%async_computation.2 | async-start | bytes 327680 | tf_op jit(solution)/shard_map/reduce_scatter | solution.py:65
  55.7 6.3 %copy-start.1 = (bf16[16,32,128]{2,1,0:T(8,128)(2,1)S(1)}, bf16[16,32,128]{2,1,0:T(8,128)(2,1)}, u32[]{:S(2)}) copy-start(bf16[16,32,128]{2,1,0:T(8,128)(2,1)} %param.11) | copy-start | bytes 393220
  55.7 6.3 %copy-start.4 = (f32[128]{0:T(128)S(1)}, f32[128]{0:T(128)}, u32[]{:S(2)}) copy-start(f32[128]{0:T(128)} %param.15) | copy-start | bytes 1540
  55.7 7.1 %copy-start.5 = (bf16[128,512]{1,0:T(8,128)(2,1)S(1)}, bf16[128,512]{1,0:T(8,128)(2,1)}, u32[]{:S(2)}) copy-start(bf16[128,512]{1,0:T(8,128)(2,1)} %param.16) | copy-start | bytes 393220
  55.7 7.1 %copy-start.6 = (f32[128]{0:T(128)S(1)}, f32[128]{0:T(128)}, u32[]{:S(2)}) copy-start(f32[128]{0:T(128)} %param.13) | copy-start | bytes 1540
  55.7 7.8 %copy-start.2 = (bf16[512,128]{1,0:T(8,128)(2,1)S(1)}, bf16[512,128]{1,0:T(8,128)(2,1)}, u32[]{:S(2)}) copy-start(bf16[512,128]{1,0:T(8,128)(2,1)} %param.17) | copy-start | bytes 393220
  55.7 7.8 %copy-start.3 = (bf16[16,32,128]{2,1,0:T(8,128)(2,1)S(1)}, bf16[16,32,128]{2,1,0:T(8,128)(2,1)}, u32[]{:S(2)}) copy-start(bf16[16,32,128]{2,1,0:T(8,128)(2,1)} %param.12) | copy-start | bytes 393220
  73.1 87.4 %reduce-scatter.5.cloned.1.call-start = ((), (), s32[]{:S(2)}) async-start(), calls=%async_computation.3 | async-start | bytes 589824 | tf_op jit(solution)/shard_map/reduce_scatter | solution.py:56
Sparse Core Ops, SparseCore 0:
  73.2 20.8 reduce-scatter.2
  97.5 63.0 reduce-scatter.4
where the time goes:
time: 169 us
  waiting for transfers between devices  80.5 us (48%)
  blocking collectives  38.6 us (23%)
  local copies, waits for them, and re-layouts  19.1 us (11%)
  between operations  14.2 us (8%)
  matrix products  12.8 us (8%)
  other arithmetic  3.45 us (2%)
    reduce_scatter x1, waiting for transfers between devices, on_device(): lax.psum_scatter(product.reshape(lax.axis_size('row') * right.shape[0], c...  65 us
    all_gather x1, blocking collectives, on_device(): right_all = lax.all_gather(right, 'row', axis=0, tiled=True)  31.8 us
    reduce_scatter x1, waiting for transfers between devices, on_device(): lax.psum_scatter(product.reshape(lax.axis_size('col') * left.shape[0], ro...  15.5 us
    all_gather x1, blocking collectives, on_device(): left_all = lax.all_gather(left, 'col', axis=0, tiled=True)  6.88 us
    convert_element_type x1, local copies, waits for them, and re-layouts, on_device(): (summed * (1.0 / SEQS)).astype(jnp.bfloat16)  6.35 us
    reshape x1, local copies, waits for them, and re-layouts, on_device(): (summed * (1.0 / SEQS)).astype(jnp.bfloat16)  6.25 us
    reshape x1, local copies, waits for them, and re-layouts, on_device(): grad_tiles = d_outer.reshape(row_count, col_count, C, C)  4.37 us
    dot_general x1, matrix products, on_device(): jnp.einsum('ijce,sic->sje', grad_tiles, left_rows, preferred_element_type...  3.42 us
  transfers between devices with their start and end apart: 2, of which 2 were waited for; matrix products, arithmetic and copies ran while one was open for 4% of the time, Pallas kernels for 0%

commit v1 on v0

v1 whole, which is shorter than its diff:
```python
import functools

import jax
import jax.numpy as jnp
from jax import lax
from jax.experimental import pallas as pl
from jax.experimental.pallas import tpu as pltpu
from jax.sharding import PartitionSpec as P

C = 32
LANES = 128
QUARTERS = LANES // C
CHUNK = 256
BF16 = jnp.bfloat16
F32 = jnp.float32
NN = (((1,), (0,)), ((), ()))
NT = (((1,), (1,)), ((), ()))


def mm(x, y, dims=NN):
    return lax.dot_general(x, y, dims, preferred_element_type=F32)


def swap_perm(major, minor):
    size = major * minor
    row = lax.broadcasted_iota(jnp.int32, (size, size), 0)
    column = lax.broadcasted_iota(jnp.int32, (size, size), 1)
    return jnp.where(column == (row % minor) * major + row // minor, 1.0, 0.0).astype(BF16)


def quarter_transpose(parts):
    turned = [x if p == 0 else pltpu.roll(x, p * C, 1) for p, x in enumerate(parts)]
    group = lax.broadcasted_iota(jnp.int32, parts[0].shape, 1) // C
    out = []
    for k in range(QUARTERS):
        y = turned[(QUARTERS - 1 - k) % QUARTERS]
        for q in range(QUARTERS - 1):
            y = jnp.where(group == q, turned[(q - k) % QUARTERS], y)
        out.append(y if k == 0 else pltpu.roll(y, LANES - k * C, 1))
    return out


def kernel(
    nrow, ncol, rows, cols,
    left_ref, right_ref, pin_ref, cot_ref, gain_ref, w_ref, bias_ref, up_ref, down_ref,
    out_ref, gl_ref, gr_ref,
    left_v, right_v, pin_v, cot_v, w_v, up_v, down_v,
    a_buf, b_buf, perm_v, permt_v, pin_p, cot_p, back_v, a_p, a_pt, o_v, out_p, d_v,
    gr_send, gr_recv, gl_acc, gl_send, gl_recv,
    load_sem, a_send_sem, a_recv_sem, b_send_sem, b_recv_sem,
    gr_send_sem, gr_recv_sem, gl_send_sem, gl_recv_sem,
):
    me_r = lax.axis_index("row")
    me_c = lax.axis_index("col")
    nch = b_buf.shape[0]
    seqs = a_p.shape[0]
    scale = 1.0 / seqs
    loads = [
        pltpu.make_async_copy(src, dst, load_sem.at[n])
        for n, (src, dst) in enumerate(
            [
                (left_ref, left_v),
                (right_ref, right_v),
                (pin_ref, pin_v),
                (cot_ref, cot_v),
                (down_ref, down_v),
                (w_ref, w_v),
                (up_ref, up_v),
            ]
        )
    ]
    for load in loads:
        load.start()

    def row_peer(d):
        return lax.rem(me_r + d, nrow)

    def col_peer(d):
        return lax.rem(me_c + d, ncol)

    barrier = pltpu.get_barrier_semaphore()
    for d in range(1, nrow):
        pl.semaphore_signal(
            barrier, inc=1, device_id=(row_peer(d), me_c), device_id_type=pl.DeviceIdType.MESH
        )
    for d in range(1, ncol):
        pl.semaphore_signal(
            barrier, inc=1, device_id=(me_r, col_peer(d)), device_id_type=pl.DeviceIdType.MESH
        )
    loads[0].wait()
    loads[1].wait()
    a_buf[me_c] = left_v[...]
    for k in range(nch):
        b_buf[k, me_r] = right_v[:, k * CHUNK:(k + 1) * CHUNK]
    pl.semaphore_wait(barrier, nrow + ncol - 2)

    def a_copy(d):
        to = col_peer(d)
        return pltpu.make_async_remote_copy(
            src_ref=left_v, dst_ref=a_buf.at[me_c],
            send_sem=a_send_sem.at[d], recv_sem=a_recv_sem.at[me_c],
            device_id=(me_r, to), device_id_type=pl.DeviceIdType.MESH,
        )

    def b_copy(k, d):
        to = row_peer(d)
        return pltpu.make_async_remote_copy(
            src_ref=right_v.at[:, k * CHUNK:(k + 1) * CHUNK], dst_ref=b_buf.at[k, me_r],
            send_sem=b_send_sem.at[k, d], recv_sem=b_recv_sem.at[k, me_r],
            device_id=(to, me_c), device_id_type=pl.DeviceIdType.MESH,
        )

    def gr_copy(k, d):
        to = row_peer(d)
        return pltpu.make_async_remote_copy(
            src_ref=gr_send.at[k, to], dst_ref=gr_recv.at[k, me_r],
            send_sem=gr_send_sem.at[k, d], recv_sem=gr_recv_sem.at[k, me_r],
            device_id=(to, me_c), device_id_type=pl.DeviceIdType.MESH,
        )

    def gl_copy(d):
        to = col_peer(d)
        return pltpu.make_async_remote_copy(
            src_ref=gl_send.at[to], dst_ref=gl_recv.at[me_c],
            send_sem=gl_send_sem.at[d], recv_sem=gl_recv_sem.at[me_c],
            device_id=(me_r, to), device_id_type=pl.DeviceIdType.MESH,
        )

    def landed(buf, sem):
        pltpu.make_async_copy(buf, buf, sem).wait()

    sends = []

    def go(copy):
        copy.start()
        sends.append(copy)

    for d in range(1, ncol):
        go(a_copy(d))
    for k in range(nch):
        for d in range(1, nrow):
            go(b_copy(k, d))

    perm_v[...] = swap_perm(C, rows)
    permt_v[...] = swap_perm(rows, C)
    if cols == C:
        pair_perm, pair_permt = perm_v[...], permt_v[...]
    else:
        pair_perm, pair_permt = swap_perm(cols, rows), swap_perm(rows, cols)
    for load in loads[2:]:
        load.wait()
    pairs = rows * cols
    width = pin_v.shape[2]
    gain = gain_ref[...].reshape(1, width)
    bias = bias_ref[...].reshape(1, width)
    pin_p[...] = mm(pair_perm, pin_v[...].reshape(pairs, width)) + bias
    cot_p[...] = mm(pair_perm, cot_v[...].reshape(pairs, width)).astype(BF16)
    back_v[...] = mm(cot_p[...], down_v[...], NT)

    for d in range(1, ncol):
        src = col_peer(d)
        landed(a_buf.at[src], a_recv_sem.at[src])
    a_all = a_buf[...].reshape(seqs, rows * C)
    a_p[...] = mm(a_all, permt_v[...]).astype(BF16)
    a_pt[...] = (mm(perm_v[...], a_all, NT) * scale).astype(BF16)

    part = CHUNK // C * rows
    tiles = CHUNK // LANES
    blocks = C // QUARTERS
    for k in range(nch):
        for d in range(1, nrow):
            src = row_peer(d)
            landed(b_buf.at[k, src], b_recv_sem.at[k, src])
        b_k = b_buf[k].reshape(seqs, CHUNK)
        m = mm(a_pt[...], b_k)
        for t in range(tiles):
            for h in range(blocks):
                r = quarter_transpose(
                    [
                        m[(h * QUARTERS + q) * rows:(h * QUARTERS + q + 1) * rows, t * LANES:(t + 1) * LANES]
                        for q in range(QUARTERS)
                    ]
                )
                for q in range(QUARTERS):
                    j = t * QUARTERS + q
                    o_v[j * rows:(j + 1) * rows, h * LANES:(h + 1) * LANES] = r[q].astype(BF16)
        span = slice(k * part, (k + 1) * part)
        middle = pin_p[span, :] + mm(o_v[...], w_v[...])
        centred = middle - jnp.mean(middle, axis=-1, keepdims=True)
        inverse = lax.rsqrt(jnp.mean(centred * centred, axis=-1, keepdims=True) + 1e-05)
        xhat = centred * inverse
        normed = (xhat * gain).astype(BF16)
        preact = mm(normed, up_v[...])
        hidden = jnp.maximum(preact, 0.0).astype(BF16)
        d_hidden = jnp.where(preact > 0.0, back_v[span, :], 0.0).astype(BF16)
        d_normed = mm(d_hidden, up_v[...], NT)
        scaled = d_normed * gain
        d_middle = cot_p[span, :].astype(F32) + inverse * (
            scaled
            - jnp.mean(scaled, axis=-1, keepdims=True)
            - xhat * jnp.mean(scaled * xhat, axis=-1, keepdims=True)
        )
        d_outer = mm(d_middle.astype(BF16), w_v[...], NT)
        for t in range(tiles):
            for h in range(blocks):
                r = quarter_transpose(
                    [
                        d_outer[(t * QUARTERS + q) * rows:(t * QUARTERS + q + 1) * rows, h * LANES:(h + 1) * LANES]
                        for q in range(QUARTERS)
                    ]
                )
                for q in range(QUARTERS):
                    c = h * QUARTERS + q
                    d_v[c * rows:(c + 1) * rows, t * LANES:(t + 1) * LANES] = r[q].astype(BF16)
        gr_send[k] = mm(a_p[...], d_v[...]).astype(BF16).reshape(gr_send.shape[1:])
        for d in range(1, nrow):
            go(gr_copy(k, d))
        gl = mm(b_k, d_v[...], NT)
        if k == 0:
            gl_acc[...] = gl
        elif k < nch - 1:
            gl_acc[...] += gl
        else:
            gl_send[...] = (gl_acc[...] + gl).astype(BF16).reshape(gl_send.shape)
            for d in range(1, ncol):
                go(gl_copy(d))
        down = mm(hidden, down_v[...])
        out_p[span, :] = (middle + down).astype(BF16)

    out_ref[...] = mm(pair_permt, out_p[...]).astype(BF16).reshape(out_ref.shape)

    for k in range(nch):
        total = gr_send[k, me_r].astype(F32)
        for d in range(1, nrow):
            src = row_peer(d)
            landed(gr_recv.at[k, src], gr_recv_sem.at[k, src])
            total = total + gr_recv[k, src].astype(F32)
        gr_ref[:, k * CHUNK:(k + 1) * CHUNK] = (total * scale).astype(BF16)
    total = gl_send[me_c].astype(F32)
    for d in range(1, ncol):
        src = col_peer(d)
        landed(gl_recv.at[src], gl_recv_sem.at[src])
        total = total + gl_recv[src].astype(F32)
    gl_ref[...] = mm((total * scale).astype(BF16), perm_v[...]).astype(BF16)
    for copy in sends:
        copy.wait_send()


def on_device(nrow, ncol, left, right, pair_in, pair_cot, ln_gain, out_weight, out_bias, trans_up, trans_down):
    rows, cols, width = pair_in.shape
    ls, lw = left.shape
    rs, rw = right.shape
    seqs = ls * ncol
    ffn = trans_up.shape[1]
    pairs = rows * cols
    nch = rw // CHUNK
    dma = pltpu.SemaphoreType.DMA
    vm = pltpu.VMEM
    scratch = [
        vm((ls, lw), BF16), vm((rs, rw), BF16),
        vm((rows, cols, width), BF16), vm((rows, cols, width), BF16),
        vm(out_weight.shape, BF16), vm(trans_up.shape, BF16), vm(trans_down.shape, BF16),
        vm((ncol, ls, lw), BF16), vm((nch, nrow, rs, CHUNK), BF16),
        vm((lw, lw), BF16), vm((lw, lw), BF16),
        vm((pairs, width), F32), vm((pairs, width), BF16), vm((pairs, ffn), F32),
        vm((seqs, lw), BF16), vm((lw, seqs), BF16),
        vm((CHUNK // C * rows, C * C), BF16), vm((pairs, width), BF16), vm((lw, CHUNK), BF16),
        vm((nch, nrow, rs, CHUNK), BF16), vm((nch, nrow, rs, CHUNK), BF16),
        vm((seqs, lw), F32), vm((ncol, ls, lw), BF16), vm((ncol, ls, lw), BF16),
        dma((7,)), dma((ncol,)), dma((ncol,)), dma((nch, nrow)), dma((nch, nrow)),
        dma((nch, nrow)), dma((nch, nrow)), dma((ncol,)), dma((ncol,)),
    ]
    hbm = pl.BlockSpec(memory_space=pl.ANY)
    vmem = pl.BlockSpec(memory_space=pltpu.VMEM)
    return pl.pallas_call(
        functools.partial(kernel, nrow, ncol, rows, cols),
        out_shape=(
            jax.ShapeDtypeStruct(pair_in.shape, BF16),
            jax.ShapeDtypeStruct(left.shape, BF16),
            jax.ShapeDtypeStruct(right.shape, BF16),
        ),
        in_specs=[hbm, hbm, hbm, hbm, vmem, hbm, vmem, hbm, hbm],
        out_specs=(vmem, vmem, vmem),
        scratch_shapes=scratch,
        compiler_params=pltpu.CompilerParams(collective_id=0, has_side_effects=True),
    )(left, right, pair_in, pair_cot, ln_gain, out_weight, out_bias, trans_up, trans_down)


def solution(mesh):
    nrow, ncol = mesh.shape["row"], mesh.shape["col"]
    return jax.shard_map(
        functools.partial(on_device, nrow, ncol),
        mesh=mesh,
        in_specs=(
            P("col", "row"),
            P("row", "col"),
            P("row", "col", None),
            P("row", "col", None),
            P(),
            P(),
            P(),
            P(),
            P(),
        ),
        out_specs=(P("row", "col", None), P("col", "row"), P("row", "col")),
        check_vma=False,
    )
```

time: 169 us -> 30.3 us (0.18)
  waiting for transfers between devices: 80.5 us -> 0 us
  blocking collectives: 38.6 us -> 0 us
  Pallas kernels: 0 us -> 26.4 us
  local copies, waits for them, and re-layouts: 19.1 us -> 2.96 us
  between operations: 14.2 us -> 0.65 us
  matrix products: 12.8 us -> 0 us
  other arithmetic: 3.45 us -> 0 us
    reduce_scatter x2 -> x0, waiting for transfers between devices: 80.5 us -> none  [the longest x1 65 us: on_device(): lax.psum_scatter(product.reshape(lax.axis_size('row') * right.shape[0], c...]
    all_gather x2 -> x0, blocking collectives: 38.6 us -> none  [the longest x1 31.8 us: on_device(): right_all = lax.all_gather(right, 'row', axis=0, tiled=True)]
    pallas_call x0 -> x1, Pallas kernels: none -> 26.4 us  [on_device(): pl.pallas_call(functools.partial(kernel, nrow, ncol, rows, cols), out_sha...]
    dot_general x8 -> x0, matrix products: 12.8 us -> none  [the longest x1 3.42 us: on_device(): jnp.einsum('ijce,sic->sje', grad_tiles, left_rows, preferred_element_type...]
    reshape x4 -> x0, local copies, waits for them, and re-layouts: 12.4 us -> none  [the longest x1 6.25 us: on_device(): (summed * (1.0 / SEQS)).astype(jnp.bfloat16)]
    convert_element_type x1 -> x0, local copies, waits for them, and re-layouts: 6.35 us -> none  [on_device(): (summed * (1.0 / SEQS)).astype(jnp.bfloat16)]
    unnamed x14 -> x7, local copies, waits for them, and re-layouts: 0.04 us -> 2.96 us
    convert_element_type x2 -> x0, other arithmetic: 2.92 us -> none  [the longest x1 1.46 us: on_device(): grad_left = (left_total * (1.0 / SEQS)).astype(jnp.bfloat16)]
  transfers between devices with their start and end apart: 2 -> 0, of which waited for: 2 -> 0; matrix products, arithmetic and copies ran while one was open for 4% -> 0% of each run, Pallas kernels for 0% -> 0%
where the time goes in v1:
time: 30.3 us; the launch traced here: 30.1 us
  Pallas kernels  26.4 us (87%)
  local copies, waits for them, and re-layouts  2.96 us (10%)
  between operations  0.65 us (2%)
    pallas_call x1, Pallas kernels, on_device(): pl.pallas_call(functools.partial(kernel, nrow, ncol, rows, cols), out_sha...  26.4 us
    unnamed x7, local copies, waits for them, and re-layouts  2.96 us

profile of v1, /device:TPU:0, one launch (start us, length us, event | category | flops | bytes accessed | tf_op | source)
XLA Modules:
  0.0 30.1 jit_solution(14206874872418526741)
XLA Ops:
  0.6 26.4 %shard_map.112 = (bf16[16,32,128]{2,1,0:T(8,128)(2,1)}, bf16[32,512]{1,0:T(8,128)(2,1)}, bf16[16,1024]{1,0:T(8,128)(2,1)}) custom-call(bf16[32,512]{1,0:T(8,128)(2,1)} %left_ref.1, bf16[16,1024]{1,0:T(8,128)(2,1)} %right_ref.1, bf16[16,32,128]{2,1,0:T(8,128)(2,1)} %pin_ref.1, bf16[16,32,128]{2,1,0:T(8,128)(2,1)} %cot_ref.1, f32[128]{0:T(128)} %gain_ref.1, ...), custom_call_target="tpu_custom_call" | custom-call | tf_op jit(solution)/shard_map/pallas_call | solution.py:275
  27.1 0.0 copy-start.1
  27.1 1.6 %copy.15 = bf16[16,32,128]{2,1,0:T(8,128)(2,1)} copy(bf16[16,32,128]{2,1,0:T(8,128)(2,1)} %get-tuple-element.6) | data formatting | bytes 262144
  28.7 0.0 copy-done.1
  28.7 0.0 copy-start
  28.7 0.6 %copy.16 = bf16[32,512]{1,0:T(8,128)(2,1)} copy(bf16[32,512]{1,0:T(8,128)(2,1)S(1)} %copy-done.1) | data formatting | bytes 65536
  29.3 0.2 copy-done
  29.4 0.6 %copy.17 = bf16[16,1024]{1,0:T(8,128)(2,1)} copy(bf16[16,1024]{1,0:T(8,128)(2,1)S(1)} %copy-done) | data formatting | bytes 65536
Async XLA Ops:
  27.1 1.6 %copy-start.1 = (bf16[32,512]{1,0:T(8,128)(2,1)S(1)}, bf16[32,512]{1,0:T(8,128)(2,1)}, u32[]{:S(2)}) copy-start(bf16[32,512]{1,0:T(8,128)(2,1)} %get-tuple-element.7) | copy-start | bytes 98308
  28.7 0.8 %copy-start = (bf16[16,1024]{1,0:T(8,128)(2,1)S(1)}, bf16[16,1024]{1,0:T(8,128)(2,1)}, u32[]{:S(2)}) copy-start(bf16[16,1024]{1,0:T(8,128)(2,1)} %get-tuple-element.8) | copy-start | bytes 98308

commit v2 on v1

--- a/solution.py
+++ b/solution.py
@@ -10,7 +10,8 @@
 C = 32
 LANES = 128
 QUARTERS = LANES // C
-CHUNK = 256
+CHUNK = 512
+LIMIT = 16 * 1024 * 1024
 BF16 = jnp.bfloat16
 F32 = jnp.float32
 NN = (((1,), (0,)), ((), ()))
@@ -44,8 +45,8 @@
     nrow, ncol, rows, cols,
     left_ref, right_ref, pin_ref, cot_ref, gain_ref, w_ref, bias_ref, up_ref, down_ref,
     out_ref, gl_ref, gr_ref,
-    left_v, right_v, pin_v, cot_v, w_v, up_v, down_v,
-    a_buf, b_buf, perm_v, permt_v, pin_p, cot_p, back_v, a_p, a_pt, o_v, out_p, d_v,
+    left_v, right_v, pin_v, cot_v, w_v, up_v, down_v, gain_v, bias_v,
+    a_buf, b_buf, perm_v, permt_v, pin_p, cot_p, back_v, a_p, a_pt, o_v, hid_v, d_v,
     gr_send, gr_recv, gl_acc, gl_send, gl_recv,
     load_sem, a_send_sem, a_recv_sem, b_send_sem, b_recv_sem,
     gr_send_sem, gr_recv_sem, gl_send_sem, gl_recv_sem,
@@ -66,6 +67,8 @@
                 (down_ref, down_v),
                 (w_ref, w_v),
                 (up_ref, up_v),
+                (gain_ref, gain_v),
+                (bias_ref, bias_v),
             ]
         )
     ]
@@ -138,7 +141,7 @@
     for d in range(1, ncol):
         go(a_copy(d))
     for k in range(nch):
-        for d in range(1, nrow):
+        for d in sorted(range(1, nrow), key=lambda d: -min(d, nrow - d)):
             go(b_copy(k, d))
 
     perm_v[...] = swap_perm(C, rows)
@@ -151,8 +154,8 @@
         load.wait()
     pairs = rows * cols
     width = pin_v.shape[2]
-    gain = gain_ref[...].reshape(1, width)
-    bias = bias_ref[...].reshape(1, width)
+    gain = gain_v[...].reshape(1, width)
+    bias = bias_v[...].reshape(1, width)
     pin_p[...] = mm(pair_perm, pin_v[...].reshape(pairs, width)) + bias
     cot_p[...] = mm(pair_perm, cot_v[...].reshape(pairs, width)).astype(BF16)
     back_v[...] = mm(cot_p[...], down_v[...], NT)
@@ -167,7 +170,7 @@
     part = CHUNK // C * rows
     tiles = CHUNK // LANES
     blocks = C // QUARTERS
-    for k in range(nch):
+    def chunk(k, carry):
         for d in range(1, nrow):
             src = row_peer(d)
             landed(b_buf.at[k, src], b_recv_sem.at[k, src])
@@ -184,7 +187,7 @@
                 for q in range(QUARTERS):
                     j = t * QUARTERS + q
                     o_v[j * rows:(j + 1) * rows, h * LANES:(h + 1) * LANES] = r[q].astype(BF16)
-        span = slice(k * part, (k + 1) * part)
+        span = pl.ds(pl.multiple_of(k * part, part), part)
         middle = pin_p[span, :] + mm(o_v[...], w_v[...])
         centred = middle - jnp.mean(middle, axis=-1, keepdims=True)
         inverse = lax.rsqrt(jnp.mean(centred * centred, axis=-1, keepdims=True) + 1e-05)
@@ -192,6 +195,8 @@
         normed = (xhat * gain).astype(BF16)
         preact = mm(normed, up_v[...])
         hidden = jnp.maximum(preact, 0.0).astype(BF16)
+        hid_v[span, :] = hidden
+        pin_p[span, :] = middle
         d_hidden = jnp.where(preact > 0.0, back_v[span, :], 0.0).astype(BF16)
         d_normed = mm(d_hidden, up_v[...], NT)
         scaled = d_normed * gain
@@ -214,20 +219,19 @@
                     d_v[c * rows:(c + 1) * rows, t * LANES:(t + 1) * LANES] = r[q].astype(BF16)
         gr_send[k] = mm(a_p[...], d_v[...]).astype(BF16).reshape(gr_send.shape[1:])
         for d in range(1, nrow):
-            go(gr_copy(k, d))
+            gr_copy(k, d).start()
         gl = mm(b_k, d_v[...], NT)
-        if k == 0:
-            gl_acc[...] = gl
-        elif k < nch - 1:
-            gl_acc[...] += gl
-        else:
-            gl_send[...] = (gl_acc[...] + gl).astype(BF16).reshape(gl_send.shape)
-            for d in range(1, ncol):
-                go(gl_copy(d))
-        down = mm(hidden, down_v[...])
-        out_p[span, :] = (middle + down).astype(BF16)
-
-    out_ref[...] = mm(pair_permt, out_p[...]).astype(BF16).reshape(out_ref.shape)
+        gl_acc[...] += gl
+        return carry
+
+    gl_acc[...] = jnp.zeros_like(gl_acc)
+    lax.fori_loop(0, nch, chunk, 0)
+    gl_send[...] = gl_acc[...].astype(BF16).reshape(gl_send.shape)
+    for d in range(1, ncol):
+        go(gl_copy(d))
+
+    out_p = (pin_p[...] + mm(hid_v[...], down_v[...])).astype(BF16)
+    out_ref[...] = mm(pair_permt, out_p).astype(BF16).reshape(out_ref.shape)
 
     for k in range(nch):
         total = gr_send[k, me_r].astype(F32)
@@ -244,6 +248,17 @@
     gl_ref[...] = mm((total * scale).astype(BF16), perm_v[...]).astype(BF16)
     for copy in sends:
         copy.wait_send()
+    for k in range(nch):
+        for d in range(1, nrow):
+            gr_copy(k, d).wait_send()
+
+
+def put_out(a, b, c, x, y, z, sem):
+    copies = [pltpu.make_async_copy(s, t, sem.at[n]) for n, (s, t) in enumerate([(a, x), (b, y), (c, z)])]
+    for copy in copies:
+        copy.start()
+    for copy in copies:
+        copy.wait()
 
 
 def on_device(nrow, ncol, left, right, pair_in, pair_cot, ln_gain, out_weight, out_bias, trans_up, trans_down):
@@ -260,30 +275,39 @@
         vm((ls, lw), BF16), vm((rs, rw), BF16),
         vm((rows, cols, width), BF16), vm((rows, cols, width), BF16),
         vm(out_weight.shape, BF16), vm(trans_up.shape, BF16), vm(trans_down.shape, BF16),
+        vm(ln_gain.shape, F32), vm(out_bias.shape, F32),
         vm((ncol, ls, lw), BF16), vm((nch, nrow, rs, CHUNK), BF16),
         vm((lw, lw), BF16), vm((lw, lw), BF16),
         vm((pairs, width), F32), vm((pairs, width), BF16), vm((pairs, ffn), F32),
         vm((seqs, lw), BF16), vm((lw, seqs), BF16),
-        vm((CHUNK // C * rows, C * C), BF16), vm((pairs, width), BF16), vm((lw, CHUNK), BF16),
+        vm((CHUNK // C * rows, C * C), BF16), vm((pairs, ffn), BF16), vm((lw, CHUNK), BF16),
         vm((nch, nrow, rs, CHUNK), BF16), vm((nch, nrow, rs, CHUNK), BF16),
         vm((seqs, lw), F32), vm((ncol, ls, lw), BF16), vm((ncol, ls, lw), BF16),
-        dma((7,)), dma((ncol,)), dma((ncol,)), dma((nch, nrow)), dma((nch, nrow)),
+        dma((9,)), dma((ncol,)), dma((ncol,)), dma((nch, nrow)), dma((nch, nrow)),
         dma((nch, nrow)), dma((nch, nrow)), dma((ncol,)), dma((ncol,)),
     ]
-    hbm = pl.BlockSpec(memory_space=pl.ANY)
+    hbm = pl.BlockSpec(memory_space=pltpu.HBM)
     vmem = pl.BlockSpec(memory_space=pltpu.VMEM)
-    return pl.pallas_call(
+    results = pl.pallas_call(
         functools.partial(kernel, nrow, ncol, rows, cols),
         out_shape=(
-            jax.ShapeDtypeStruct(pair_in.shape, BF16),
-            jax.ShapeDtypeStruct(left.shape, BF16),
-            jax.ShapeDtypeStruct(right.shape, BF16),
+            pltpu.VMEM(pair_in.shape, BF16),
+            pltpu.VMEM(left.shape, BF16),
+            pltpu.VMEM(right.shape, BF16),
         ),
-        in_specs=[hbm, hbm, hbm, hbm, vmem, hbm, vmem, hbm, hbm],
+        in_specs=[hbm] * 9,
         out_specs=(vmem, vmem, vmem),
         scratch_shapes=scratch,
         compiler_params=pltpu.CompilerParams(collective_id=0, has_side_effects=True),
     )(left, right, pair_in, pair_cot, ln_gain, out_weight, out_bias, trans_up, trans_down)
+    return pl.pallas_call(
+        put_out,
+        out_shape=tuple(jax.ShapeDtypeStruct(x.shape, x.dtype) for x in results),
+        in_specs=[vmem] * 3,
+        out_specs=(hbm, hbm, hbm),
+        scratch_shapes=[dma((3,))],
+        compiler_params=pltpu.CompilerParams(vmem_limit_bytes=LIMIT // 8),
+    )(*results)
 
 
 def solution(mesh):

time: 30.3 us -> 23.3 us (0.77)
  Pallas kernels: 26.4 us -> 22.5 us
  local copies, waits for them, and re-layouts: 2.96 us -> 0 us
    pallas_call x1, Pallas kernels: 26.4 us -> 21.8 us  [on_device(): pl.pallas_call(functools.partial(kernel, nrow, ncol, rows, cols), out_sha...]
    unnamed x7 -> x0, local copies, waits for them, and re-layouts: 2.96 us -> none
    pallas_call x0 -> x1, Pallas kernels: none -> 0.7 us  [on_device(): pl.pallas_call(put_out, out_shape=tuple((jax.ShapeDtypeStruct(x.shape, x....]
where the time goes in v2:
time: 23.3 us; the launch traced here: 23.2 us
  Pallas kernels  22.5 us (97%)
  between operations  0.64 us (3%)
    pallas_call x1, Pallas kernels, on_device(): pl.pallas_call(functools.partial(kernel, nrow, ncol, rows, cols), out_sha...  21.8 us
    pallas_call x1, Pallas kernels, on_device(): pl.pallas_call(put_out, out_shape=tuple((jax.ShapeDtypeStruct(x.shape, x....  0.7 us

profile of v2, /device:TPU:0, one launch (start us, length us, event | category | flops | bytes accessed | tf_op | source)
XLA Modules:
  0.0 23.2 jit_solution(8361103868188946489)
XLA Ops:
  0.6 21.8 %shard_map.112 = (bf16[16,32,128]{2,1,0:T(8,128)(2,1)S(1)}, bf16[32,512]{1,0:T(8,128)(2,1)S(1)}, bf16[16,1024]{1,0:T(8,128)(2,1)S(1)}) custom-call(bf16[32,512]{1,0:T(8,128)(2,1)} %left_ref.1, bf16[16,1024]{1,0:T(8,128)(2,1)} %right_ref.1, bf16[16,32,128]{2,1,0:T(8,128)(2,1)} %pin_ref.1, bf16[16,32,128]{2,1,0:T(8,128)(2,1)} %cot_ref.1, f32[128]{0:T(128)} %gain_ref.1, ...), custom_call_target="tpu_custom_call" | custom-call | tf_op jit(solution)/shard_map/pallas_call | solution.py:291
  22.5 0.7 %shard_map.113 = (bf16[16,32,128]{2,1,0:T(8,128)(2,1)}, bf16[32,512]{1,0:T(8,128)(2,1)}, bf16[16,1024]{1,0:T(8,128)(2,1)}) custom-call(bf16[16,32,128]{2,1,0:T(8,128)(2,1)S(1)} %get-tuple-element.6.a, bf16[32,512]{1,0:T(8,128)(2,1)S(1)} %get-tuple-element.7.b, bf16[16,1024]{1,0:T(8,128)(2,1)S(1)} %get-tuple-element.8.c), custom_call_target="tpu_custom_call" | custom-call | tf_op jit(solution)/shard_map/pallas_call | solution.py:303
